TPU v7x, 32 devices: a whole 2x2x4 slice. The times are simulated.
32 devices in a mesh: lon: 8 (over y, x, core), lat: 4 (over z).
Axes of the slice: x: 2, y: 2, z: 4, core: 2. Of those that a mesh axis runs over, the one named last changes fastest.
Arguments:
- fields: bfloat16 [32, 256, 256], P('lat', 'lon'), may hold values from -6 to 6
- norm_lon: float32 [256], replicated, may hold values from 0.25 to 1.75
- query_lon: bfloat16 [256, 256], replicated, may hold values from -0.375 to 0.375
- key_lon: bfloat16 [256, 256], replicated, may hold values from -0.375 to 0.375
- value_lon: bfloat16 [256, 256], replicated, may hold values from -0.375 to 0.375
- out_lon: bfloat16 [256, 256], replicated, may hold values from -0.375 to 0.375
- temp_lon: float32 [8], replicated, may hold values from 0.5 to 12
- bias_lon: float32 [8], replicated, may hold values from -2 to 2
- norm_lat: float32 [256], replicated, may hold values from 0.25 to 1.75
- query_lat: bfloat16 [256, 256], replicated, may hold values from -0.375 to 0.375
- key_lat: bfloat16 [256, 256], replicated, may hold values from -0.375 to 0.375
- value_lat: bfloat16 [256, 256], replicated, may hold values from -0.375 to 0.375
- out_lat: bfloat16 [256, 256], replicated, may hold values from -0.375 to 0.375
- temp_lat: float32 [8], replicated, may hold values from 0.5 to 12
- bias_lat: float32 [8], replicated, may hold values from -4 to 0
- norm_mlp: float32 [256], replicated, may hold values from 0.25 to 1.75
- w_gate: bfloat16 [256, 1024], replicated, may hold values from -0.375 to 0.375
- w_up: bfloat16 [256, 1024], replicated, may hold values from -0.375 to 0.375
- w_down: bfloat16 [1024, 256], replicated, may hold values from -0.1875 to 0.1875
Outputs:
- updated: bfloat16 [32, 256, 256], P('lat', 'lon')
All inputs are finite; a program needn't handle non-finite values.
Results may differ from a plain program's by a relative error of at most 0.018.
The roundings to bfloat16 on the way count: a program that leaves them out, or rounds other values in their place, can miss the bound.
Values may be sent and summed in bfloat16 or wider, within the bound.
A program may use at most 64 MiB of HBM per device.

v0:
```python
import math
import jax
import jax.numpy as jnp
from jax import lax
from jax.sharding import PartitionSpec as P


def normalize(values, gain):
    factor = lax.rsqrt(jnp.mean(values * values, axis=-1, keepdims=True) + 1e-06)
    return (values * factor * gain).astype(jnp.bfloat16)


def project(values, weight):
    return jnp.dot(values, weight, preferred_element_type=jnp.float32).astype(jnp.bfloat16)


def attend_lat(queries, keys, values, temp, bias):
    count, cols, depth = queries.shape
    heads = temp.shape[0]
    size = depth // heads
    qh = queries.reshape(count, cols, heads, size)
    kh = keys.reshape(count, cols, heads, size)
    vh = values.reshape(count, cols, heads, size)
    scores = jnp.einsum("ichd,jchd->chij", qh, kh, preferred_element_type=jnp.float32)
    place = jnp.arange(count, dtype=jnp.int32)
    spread = jnp.abs(place[:, None] - place[None, :]).astype(jnp.float32) / count
    scores = (
        scores * (temp / math.sqrt(size))[None, :, None, None]
        + bias[None, :, None, None] * spread[None, None]
    )
    expo = jnp.exp(scores - jnp.max(scores, axis=-1, keepdims=True))
    denom = jnp.sum(expo, axis=-1)
    mixed = jnp.einsum(
        "chij,jchd->ichd", expo.astype(jnp.bfloat16), vh, preferred_element_type=jnp.float32
    )
    mixed = mixed / jnp.transpose(denom, (2, 0, 1))[..., None]
    return mixed.astype(jnp.bfloat16).reshape(count, cols, depth)


def body(
    fields,
    norm_lon,
    query_lon,
    key_lon,
    value_lon,
    out_lon,
    temp_lon,
    bias_lon,
    norm_lat,
    query_lat,
    key_lat,
    value_lat,
    out_lat,
    temp_lat,
    bias_lat,
    norm_mlp,
    w_gate,
    w_up,
    w_down,
):
    rows, width, depth = fields.shape
    heads = temp_lon.shape[0]
    size = depth // heads
    total_lon = width * lax.axis_size("lon")
    resid = fields.astype(jnp.float32)
    normed = normalize(resid, norm_lon)
    scale_lon = temp_lon / math.sqrt(size)
    query_place = lax.axis_index("lon") * width + jnp.arange(width, dtype=jnp.int32)
    queries = project(normed, query_lon).reshape(rows, width, heads, size)
    piece = lax.all_gather(normed, "lon", axis=1, tiled=True)
    keys = project(piece, key_lon)
    count = keys.shape[1]
    key_place = jnp.arange(count, dtype=jnp.int32)
    angle = (query_place[:, None] - key_place[None, :]).astype(jnp.float32) * (
        2.0 * math.pi / total_lon
    )
    wave = jnp.cos(angle)

    def one_row(items):
        query_row, key_row, value_row, peak, total, accum = items
        key_heads = key_row.reshape(count, heads, size)
        value_heads = value_row.reshape(count, heads, size)
        scores = jnp.einsum(
            "ihd,jhd->hij", query_row, key_heads, preferred_element_type=jnp.float32
        )
        scores = scores * scale_lon[:, None, None] + bias_lon[:, None, None] * wave[None]
        fresh = jnp.maximum(peak, jnp.max(scores, axis=-1))
        shrink = jnp.exp(peak - fresh)
        expo = jnp.exp(scores - fresh[..., None])
        total = total * shrink + jnp.sum(expo, axis=-1)
        mixed = jnp.einsum(
            "hij,jhd->ihd",
            expo.astype(jnp.bfloat16),
            value_heads,
            preferred_element_type=jnp.float32,
        )
        accum = accum.reshape(width, heads, size) * jnp.transpose(shrink)[:, :, None] + mixed
        return (fresh, total, accum.reshape(width, depth))

    peak = jnp.full((rows, heads, width), -1e30, jnp.float32)
    total = jnp.zeros((rows, heads, width), jnp.float32)
    accum = jnp.zeros((rows, width, depth), jnp.float32)
    peak, total, accum = lax.map(
        one_row, (queries, keys, project(piece, value_lon), peak, total, accum)
    )
    attended = accum.reshape(rows, width, heads, size) / jnp.transpose(total, (0, 2, 1))[..., None]
    attended = attended.astype(jnp.bfloat16).reshape(rows, width, depth)
    first = resid + jnp.dot(attended, out_lon, preferred_element_type=jnp.float32)
    normed_lat = normalize(first, norm_lat)
    query_col = project(normed_lat, query_lat)
    key_col = project(normed_lat, key_lat)
    value_col = project(normed_lat, value_lat)
    query_col, key_col, value_col = (
        lax.all_to_all(query_col, "lat", split_axis=1, concat_axis=0, tiled=True),
        lax.all_to_all(key_col, "lat", split_axis=1, concat_axis=0, tiled=True),
        lax.all_to_all(value_col, "lat", split_axis=1, concat_axis=0, tiled=True),
    )
    mixed_lat = attend_lat(query_col, key_col, value_col, temp_lat, bias_lat)
    returned = lax.all_to_all(mixed_lat, "lat", split_axis=0, concat_axis=1, tiled=True)
    second = first + jnp.dot(returned, out_lat, preferred_element_type=jnp.float32)
    normed_mlp = normalize(second, norm_mlp)
    gate = jnp.dot(normed_mlp, w_gate, preferred_element_type=jnp.float32)
    upper = jnp.dot(normed_mlp, w_up, preferred_element_type=jnp.float32)
    hidden = (jax.nn.silu(gate) * upper).astype(jnp.bfloat16)
    return (second + jnp.dot(hidden, w_down, preferred_element_type=jnp.float32)).astype(
        jnp.bfloat16
    )


def solution(mesh):
    in_specs = (
        P("lat", "lon", None),
        P(),
        P(),
        P(),
        P(),
        P(),
        P(),
        P(),
        P(),
        P(),
        P(),
        P(),
        P(),
        P(),
        P(),
        P(),
        P(),
        P(),
        P(),
    )
    out_specs = P("lat", "lon", None)
    return jax.shard_map(body, mesh=mesh, in_specs=in_specs, out_specs=out_specs, check_vma=False)
```

profile of v0, /device:TPU:0, one launch (start us, length us, event | category | flops | bytes accessed | tf_op | source)
XLA Modules:
  0.0 112.4 jit_solution(1554158160764497591)
XLA Ops:
  6.6 1.1 fusion.35
  7.7 1.7 %fusion.37 = bf16[8,32,256]{2,1,0:T(8,128)(2,1)} fusion(bf16[8,32,256]{2,1,0:T(8,128)(2,1)} %param.21, f32[256]{0:T(256)} %param.22, f32[8,32]{1,0:T(8,128)S(1)} %add_rsqrt_fusion.2), kind=kLoop, calls=%fused_computation.60 | loop fusion | flops 262144 | bytes 264192 | tf_op jit(solution)/shard_map/convert_element_type | solution.py:10
  9.4 1.2 %convolution_convert_fusion.5 = bf16[8,32,256]{2,1,0:T(8,128)(2,1)S(1)} fusion(bf16[8,32,256]{2,1,0:T(8,128)(2,1)} %fusion.37, bf16[256,256]{1,0:T(8,128)(2,1)} %param.23), kind=kOutput, calls=%fused_computation.36 | convolution fusion | flops 33619968 | bytes 393216 | tf_op jit(solution)/shard_map/dot_general | solution.py:14
  10.6 1.0 reshape.126
  11.7 23.9 %all-gather.2.cloned.1.call-done = bf16[8,256,256]{2,1,0:T(8,128)(2,1)} async-done(((bf16[8,32,256]{2,1,0:T(8,128)(2,1)}), bf16[8,256,256]{2,1,0:T(8,128)(2,1)}) %all-gather.2.cloned.1.call-update) | async-done | bytes 1048592 | tf_op jit(solution)/shard_map/all_gather | solution.py:70
  35.6 1.7 %convolution_convert_fusion.1 = bf16[8,256,256]{2,1,0:T(8,128)(2,1)S(1)} fusion(bf16[8,256,256]{2,1,0:T(8,128)(2,1)} %all-gather.2.cloned.1.call-done, bf16[256,256]{1,0:T(8,128)(2,1)S(1)} %copy-done.3), kind=kOutput, calls=%fused_computation.20 | convolution fusion | flops 268959744 | bytes 2228224 | tf_op jit(solution)/shard_map/dot_general | solution.py:14
  37.4 0.4 convolution_convert_fusion
  38.1 21.5 %while.13 = (s32[]{:T(128)}, f32[8,8,32]{2,1,0:T(8,128)S(1)}, f32[8,32,256]{1,2,0:T(8,128)}, bf16[8,32,8,32]{3,2,1,0:T(8,128)(2,1)}, bf16[8,256,256]{2,1,0:T(8,1...) while((s32[]{:T(128)}, f32[8,8,32]{2,1,0:T(8,128)S(1)}, ...), condition=%wide.region_4.5_spmd.clone, body=%wide.region_1.4_spmd.clone.sunk | while | flops 8946946 | bytes 2429245 | solution.py:103
  38.4 0.9 constant_dynamic-slice_fusion.6
  39.8 0.2 fusion.79
  40.1 0.7 constant_dynamic-update-slice_fusion.2
  41.1 0.9 constant_dynamic-slice_fusion.6
  42.5 0.2 fusion.79
  42.8 0.7 constant_dynamic-update-slice_fusion.2
  43.8 0.9 constant_dynamic-slice_fusion.6
  45.2 0.2 fusion.79
  45.5 0.7 constant_dynamic-update-slice_fusion.2
  46.5 0.9 constant_dynamic-slice_fusion.6
  47.9 0.2 fusion.79
  48.1 0.7 constant_dynamic-update-slice_fusion.2
  49.1 0.9 constant_dynamic-slice_fusion.6
  50.8 0.7 constant_dynamic-update-slice_fusion.2
  51.8 0.9 constant_dynamic-slice_fusion.6
  53.5 0.7 constant_dynamic-update-slice_fusion.2
  54.5 0.9 constant_dynamic-slice_fusion.6
  56.2 0.7 constant_dynamic-update-slice_fusion.2
  57.2 0.9 constant_dynamic-slice_fusion.6
  58.9 0.7 constant_dynamic-update-slice_fusion.2
  59.5 1.4 %fusion.16 = bf16[8,32,256]{1,2,0:T(8,128)(2,1)S(1)} fusion(f32[8,32,256]{1,2,0:T(8,128)} %get-tuple-element.53, f32[8,32,8]{1,2,0:T(8,128)S(1)} %bitcast.131), kind=kLoop, calls=%fused_computation.38 | loop fusion | flops 131072 | bytes 401408 | tf_op jit(solution)/shard_map/convert_element_type | solution.py:107
  61.0 0.4 multiply_reduce_fusion.1
  61.5 0.3 copy-done.5
  62.0 0.7 copy.48
  62.8 4.7 %all-to-all-start.2 = ((bf16[8,32,256]{2,0,1:T(8,128)(2,1)}), bf16[8,32,256]{2,0,1:T(8,128)(2,1)S(1)}, u32[]{:S(2)}, u32[]{:S(2)}) async-start(bf16[8,32,256]{2,0,1:T(8,128)(2,1)} %copy.48), calls=%async_computation.2 | async-start | bytes 262144 | tf_op jit(solution)/shard_map/all_to_all | solution.py:115
  67.7 0.7 copy.46
  68.4 5.4 %all-to-all-done.2 = bf16[8,32,256]{2,0,1:T(8,128)(2,1)S(1)} async-done(((bf16[8,32,256]{2,0,1:T(8,128)(2,1)}), bf16[8,32,256]{2,0,1:T(8,128)(2,1)S(1)}, u32[]{:S(2)}, u32[]{:S(2)}) %all-to-all-start.2) | async-done | bytes 131104 | tf_op jit(solution)/shard_map/all_to_all | solution.py:115
  73.8 3.3 %all-to-all-start.1 = ((bf16[8,32,256]{2,0,1:T(8,128)(2,1)}), bf16[8,32,256]{2,0,1:T(8,128)(2,1)S(1)}, u32[]{:S(2)}, u32[]{:S(2)}) async-start(bf16[8,32,256]{2,0,1:T(8,128)(2,1)} %copy.46), calls=%async_computation.1 | async-start | bytes 262144 | tf_op jit(solution)/shard_map/all_to_all | solution.py:114
  77.3 0.7 copy.44
  78.0 5.0 %all-to-all-done.1 = bf16[8,32,256]{2,0,1:T(8,128)(2,1)S(1)} async-done(((bf16[8,32,256]{2,0,1:T(8,128)(2,1)}), bf16[8,32,256]{2,0,1:T(8,128)(2,1)S(1)}, u32[]{:S(2)}, u32[]{:S(2)}) %all-to-all-start.1) | async-done | bytes 131104 | tf_op jit(solution)/shard_map/all_to_all | solution.py:114
  83.0 3.3 %all-to-all-start = ((bf16[8,32,256]{2,0,1:T(8,128)(2,1)}), bf16[8,32,256]{2,0,1:T(8,128)(2,1)S(1)}, u32[]{:S(2)}, u32[]{:S(2)}) async-start(bf16[8,32,256]{2,0,1:T(8,128)(2,1)} %copy.44), calls=%async_computation | async-start | bytes 262144 | tf_op jit(solution)/shard_map/all_to_all | solution.py:116
  86.9 5.3 %all-to-all-done = bf16[8,32,256]{2,0,1:T(8,128)(2,1)S(1)} async-done(((bf16[8,32,256]{2,0,1:T(8,128)(2,1)}), bf16[8,32,256]{2,0,1:T(8,128)(2,1)S(1)}, u32[]{:S(2)}, u32[]{:S(2)}) %all-to-all-start) | async-done | bytes 131104 | tf_op jit(solution)/shard_map/all_to_all | solution.py:116
  92.5 0.9 fusion.56
  93.4 0.3 fusion.22
  93.7 0.6 fusion.11
  94.5 8.4 %all_to_all.63 = bf16[32,8,256]{2,1,0:T(8,128)(2,1)S(1)} all-to-all(bf16[32,8,256]{2,1,0:T(8,128)(2,1)S(1)} %copy.54), channel_id=1, replica_groups=mesh['lon'=8,'lat'=4] {'lat'}, dimensions={0} | all-to-all | bytes 262144 | tf_op jit(solution)/shard_map/all_to_all | solution.py:119
  102.9 0.3 multiply_reduce_fusion
  103.2 0.3 fusion.28
  103.5 0.6 copy-done.14
  104.4 1.2 %fusion.15 = bf16[8,32,256]{2,1,0:T(8,128)(2,1)} fusion(f32[8,32,256]{2,1,0:T(8,128)S(1)} %get-tuple-element.132, f32[8,32,1024]{2,1,0:T(8,128)S(1)} %fusion.28, bf16[1024,256]{1,0:T(8,128)(2,1)S(1)} %copy-done.14, bf16[256,1024]{1,0:T(8,128)(2,1)S(1)} %copy-done.15, f32[256]{0:T(256)S(1)} %copy-done.12, f32[8,32]{1,0:T(8,128)S(1)} %add_rsqrt_fusion), kind=kOutput, calls=%fused_computation.32 | convolution fusion | flops 270336000 | bytes 2492416 | tf_op jit(solution)/shard_map/dot_general | solution.py:125
  (125 shorter events, 10.2 us)
Async XLA Ops:
  6.5 96.7 %copy-start = (bf16[256,1024]{1,0:T(8,128)(2,1)S(1)}, bf16[256,1024]{1,0:T(8,128)(2,1)}, u32[]{:S(2)}) copy-start(bf16[256,1024]{1,0:T(8,128)(2,1)} %param.37) | copy-start | bytes 1572868
  6.5 5.1 %copy-start.16 = (f32[8]{0:T(128)S(1)}, f32[8]{0:T(128)}, u32[]{:S(2)}) copy-start(f32[8]{0:T(128)} %param.27) | copy-start | bytes 100
  6.5 5.1 %copy-start.13 = (f32[8]{0:T(128)S(1)}, f32[8]{0:T(128)}, u32[]{:S(2)}) copy-start(f32[8]{0:T(128)} %param.35) | copy-start | bytes 100
  6.5 29.1 %copy-start.3 = (bf16[256,256]{1,0:T(8,128)(2,1)S(1)}, bf16[256,256]{1,0:T(8,128)(2,1)}, u32[]{:S(2)}) copy-start(bf16[256,256]{1,0:T(8,128)(2,1)} %param.24) | copy-start | bytes 393220
  6.5 29.1 %all-gather.2.cloned.1.call-start = ((), (), s32[]{:S(2)}) async-start(), calls=%async_computation.4 | async-start | bytes 1179648 | tf_op jit(solution)/shard_map/all_gather | solution.py:70
  11.7 25.7 %copy-start.4 = (bf16[256,256]{1,0:T(8,128)(2,1)S(1)}, bf16[256,256]{1,0:T(8,128)(2,1)}, u32[]{:S(2)}) copy-start(bf16[256,256]{1,0:T(8,128)(2,1)} %param.25) | copy-start | bytes 393220
  35.6 1.8 %copy-start.1 = (bf16[8,256,256]{2,1,0:T(8,128)(2,1)S(1)}, bf16[8,256,256]{2,1,0:T(8,128)(2,1)}, u32[]{:S(2)}) copy-start(bf16[8,256,256]{2,1,0:T(8,128)(2,1)} %all-gather.2.cloned.1.call-done) | copy-start | bytes 3145732
  37.4 0.7 copy-start.10
  59.5 1.4 %copy-start.2 = (bf16[8,32,256]{2,1,0:T(8,128)(2,1)S(1)}, bf16[8,32,256]{2,1,0:T(8,128)(2,1)}, u32[]{:S(2)}) copy-start(bf16[8,32,256]{2,1,0:T(8,128)(2,1)} %param.21) | copy-start | bytes 393220
  59.5 1.4 %copy-start.9 = (bf16[256,256]{1,0:T(8,128)(2,1)S(1)}, bf16[256,256]{1,0:T(8,128)(2,1)}, u32[]{:S(2)}) copy-start(bf16[256,256]{1,0:T(8,128)(2,1)} %param.26) | copy-start | bytes 393220
  59.5 1.8 %copy-start.11 = (f32[256]{0:T(256)S(1)}, f32[256]{0:T(256)}, u32[]{:S(2)}) copy-start(f32[256]{0:T(256)} %param.29) | copy-start | bytes 3076
  60.9 0.9 copy-start.5
  60.9 6.5 %copy-start.6 = (bf16[256,256]{1,0:T(8,128)(2,1)S(1)}, bf16[256,256]{1,0:T(8,128)(2,1)}, u32[]{:S(2)}) copy-start(bf16[256,256]{1,0:T(8,128)(2,1)} %param.30) | copy-start | bytes 393220
  61.4 15.7 %copy-start.7 = (bf16[256,256]{1,0:T(8,128)(2,1)S(1)}, bf16[256,256]{1,0:T(8,128)(2,1)}, u32[]{:S(2)}) copy-start(bf16[256,256]{1,0:T(8,128)(2,1)} %param.32) | copy-start | bytes 393220
  62.8 23.6 %copy-start.17 = (f32[8]{0:T(128)S(1)}, f32[8]{0:T(128)}, u32[]{:S(2)}) copy-start(f32[8]{0:T(128)} %param.34) | copy-start | bytes 100
  62.8 11.0 %all-to-all-start.2 = ((bf16[8,32,256]{2,0,1:T(8,128)(2,1)}), bf16[8,32,256]{2,0,1:T(8,128)(2,1)S(1)}, u32[]{:S(2)}, u32[]{:S(2)}) async-start(bf16[8,32,256]{2,0,1:T(8,128)(2,1)} %copy.48), calls=%async_computation.2 | async-start | bytes 262144 | tf_op jit(solution)/shard_map/all_to_all | solution.py:115
  73.8 9.2 %all-to-all-start.1 = ((bf16[8,32,256]{2,0,1:T(8,128)(2,1)}), bf16[8,32,256]{2,0,1:T(8,128)(2,1)S(1)}, u32[]{:S(2)}, u32[]{:S(2)}) async-start(bf16[8,32,256]{2,0,1:T(8,128)(2,1)} %copy.46), calls=%async_computation.1 | async-start | bytes 262144 | tf_op jit(solution)/shard_map/all_to_all | solution.py:114
  83.0 9.2 %all-to-all-start = ((bf16[8,32,256]{2,0,1:T(8,128)(2,1)}), bf16[8,32,256]{2,0,1:T(8,128)(2,1)S(1)}, u32[]{:S(2)}, u32[]{:S(2)}) async-start(bf16[8,32,256]{2,0,1:T(8,128)(2,1)} %copy.44), calls=%async_computation | async-start | bytes 262144 | tf_op jit(solution)/shard_map/all_to_all | solution.py:116
  93.6 9.2 %copy-start.8 = (bf16[256,256]{1,0:T(8,128)(2,1)S(1)}, bf16[256,256]{1,0:T(8,128)(2,1)}, u32[]{:S(2)}) copy-start(bf16[256,256]{1,0:T(8,128)(2,1)} %param.33) | copy-start | bytes 393220
  94.2 9.0 %copy-start.12 = (f32[256]{0:T(256)S(1)}, f32[256]{0:T(256)}, u32[]{:S(2)}) copy-start(f32[256]{0:T(256)} %param.36) | copy-start | bytes 3076
  103.1 1.0 copy-start.14
  103.2 1.2 %copy-start.15 = (bf16[256,1024]{1,0:T(8,128)(2,1)S(1)}, bf16[256,1024]{1,0:T(8,128)(2,1)}, u32[]{:S(2)}) copy-start(bf16[256,1024]{1,0:T(8,128)(2,1)} %param.38) | copy-start | bytes 1572868
Sparse Core Ops, SparseCore 0:
  9.5 26.0 all-gather.1
where the time goes:
time: 113 us; the launch traced here: 112 us
  waiting for transfers between devices  39.5 us (35%)
  local copies, waits for them, and re-layouts  19.6 us (17%)
  between operations  13.8 us (12%)
  starting transfers between devices  11.4 us (10%)
  matrix products  11.4 us (10%)
  blocking collectives  8.41 us (7%)
  other arithmetic  7.81 us (7%)
    all_gather x1, waiting for transfers between devices, body(): piece = lax.all_gather(normed, 'lon', axis=1, tiled=True)  23.9 us
    dynamic_slice x32, local copies, waits for them, and re-layouts, body(): lax.map(one_row, (queries, keys, project(piece, value_lon), peak, total,...  8.61 us
    all_to_all x1, blocking collectives, body(): lax.all_to_all(mixed_lat, 'lat', split_axis=0, concat_axis=1, tiled=True)  8.41 us
    all_to_all x1, waiting for transfers between devices, body(): lax.all_to_all(key_col, 'lat', split_axis=1, concat_axis=0, tiled=True)  5.37 us
    all_to_all x1, waiting for transfers between devices, body(): lax.all_to_all(value_col, 'lat', split_axis=1, concat_axis=0, tiled=True)  5.31 us
    dynamic_update_slice x8, local copies, waits for them, and re-layouts, body(): lax.map(one_row, (queries, keys, project(piece, value_lon), peak, total,...  5.3 us
    all_to_all x1, waiting for transfers between devices, body(): lax.all_to_all(query_col, 'lat', split_axis=1, concat_axis=0, tiled=True)  4.95 us
    all_to_all x1, starting transfers between devices, body(): lax.all_to_all(key_col, 'lat', split_axis=1, concat_axis=0, tiled=True)  4.72 us
  transfers between devices with their start and end apart: 4, of which 4 were waited for; matrix products, arithmetic and copies ran while one was open for 4% of the time, Pallas kernels for 0%

commit v1 on v0

--- a/solution.py
+++ b/solution.py
@@ -116,7 +116,10 @@
         lax.all_to_all(value_col, "lat", split_axis=1, concat_axis=0, tiled=True),
     )
     mixed_lat = attend_lat(query_col, key_col, value_col, temp_lat, bias_lat)
-    returned = lax.all_to_all(mixed_lat, "lat", split_axis=0, concat_axis=1, tiled=True)
+    returned = jnp.concatenate(
+        lax.all_to_all(jnp.stack(jnp.split(mixed_lat, lax.axis_size("lat"), axis=0)), "lat", 0, 0),
+        axis=1,
+    )
     second = first + jnp.dot(returned, out_lat, preferred_element_type=jnp.float32)
     normed_mlp = normalize(second, norm_mlp)
     gate = jnp.dot(normed_mlp, w_gate, preferred_element_type=jnp.float32)

time: 113 us -> 114 us (level)
  no operation moved by 1% of the time
where the time goes in v1:
time: 114 us; the launch traced here: 113 us
  waiting for transfers between devices  39.5 us (35%)
  local copies, waits for them, and re-layouts  20.1 us (18%)
  between operations  13.8 us (12%)
  matrix products  11.6 us (10%)
  starting transfers between devices  11.4 us (10%)
  blocking collectives  8.41 us (7%)
  other arithmetic  7.85 us (7%)
    all_gather x1, waiting for transfers between devices, body(): piece = lax.all_gather(normed, 'lon', axis=1, tiled=True)  23.9 us
    dynamic_slice x32, local copies, waits for them, and re-layouts, body(): lax.map(one_row, (queries, keys, project(piece, value_lon), peak, total,...  8.61 us
    all_to_all x1, blocking collectives, body(): lax.all_to_all(jnp.stack(jnp.split(mixed_lat, lax.axis_size('lat'), axis=...  8.41 us
    all_to_all x1, waiting for transfers between devices, body(): lax.all_to_all(key_col, 'lat', split_axis=1, concat_axis=0, tiled=True)  5.37 us
    dynamic_update_slice x8, local copies, waits for them, and re-layouts, body(): lax.map(one_row, (queries, keys, project(piece, value_lon), peak, total,...  5.31 us
    all_to_all x1, waiting for transfers between devices, body(): lax.all_to_all(value_col, 'lat', split_axis=1, concat_axis=0, tiled=True)  5.31 us
    all_to_all x1, waiting for transfers between devices, body(): lax.all_to_all(query_col, 'lat', split_axis=1, concat_axis=0, tiled=True)  4.95 us
    all_to_all x1, starting transfers between devices, body(): lax.all_to_all(key_col, 'lat', split_axis=1, concat_axis=0, tiled=True)  4.73 us
  transfers between devices with their start and end apart: 4, of which 4 were waited for; matrix products, arithmetic and copies ran while one was open for 4% of the time, Pallas kernels for 0%

profile of v1, /device:TPU:0, one launch (start us, length us, event | category | flops | bytes accessed | tf_op | source)
XLA Modules:
  0.0 113.2 jit_solution(10143421632284966262)
XLA Ops:
  6.6 1.1 fusion.35
  7.7 1.7 %fusion.37 = bf16[8,32,256]{2,1,0:T(8,128)(2,1)} fusion(bf16[8,32,256]{2,1,0:T(8,128)(2,1)} %param.21, f32[256]{0:T(256)} %param.22, f32[8,32]{1,0:T(8,128)S(1)} %add_rsqrt_fusion.2), kind=kLoop, calls=%fused_computation.60 | loop fusion | flops 262144 | bytes 264192 | tf_op jit(solution)/shard_map/convert_element_type | solution.py:10
  9.4 1.2 %convolution_convert_fusion.5 = bf16[8,32,256]{2,1,0:T(8,128)(2,1)S(1)} fusion(bf16[8,32,256]{2,1,0:T(8,128)(2,1)} %fusion.37, bf16[256,256]{1,0:T(8,128)(2,1)} %param.23), kind=kOutput, calls=%fused_computation.36 | convolution fusion | flops 33619968 | bytes 393216 | tf_op jit(solution)/shard_map/dot_general | solution.py:14
  10.6 1.0 reshape.138
  11.7 23.9 %all-gather.2.cloned.1.call-done = bf16[8,256,256]{2,1,0:T(8,128)(2,1)} async-done(((bf16[8,32,256]{2,1,0:T(8,128)(2,1)}), bf16[8,256,256]{2,1,0:T(8,128)(2,1)}) %all-gather.2.cloned.1.call-update) | async-done | bytes 1048592 | tf_op jit(solution)/shard_map/all_gather | solution.py:70
  35.6 1.7 %convolution_convert_fusion.1 = bf16[8,256,256]{2,1,0:T(8,128)(2,1)S(1)} fusion(bf16[8,256,256]{2,1,0:T(8,128)(2,1)} %all-gather.2.cloned.1.call-done, bf16[256,256]{1,0:T(8,128)(2,1)S(1)} %copy-done.3), kind=kOutput, calls=%fused_computation.20 | convolution fusion | flops 268959744 | bytes 2228224 | tf_op jit(solution)/shard_map/dot_general | solution.py:14
  37.4 0.4 convolution_convert_fusion
  38.1 21.5 %while.13 = (s32[]{:T(128)}, f32[8,8,32]{2,1,0:T(8,128)S(1)}, f32[8,32,256]{1,2,0:T(8,128)}, bf16[8,32,8,32]{3,2,1,0:T(8,128)(2,1)}, bf16[8,256,256]{2,1,0:T(8,1...) while((s32[]{:T(128)}, f32[8,8,32]{2,1,0:T(8,128)S(1)}, ...), condition=%wide.region_4.5_spmd.clone, body=%wide.region_1.4_spmd.clone.sunk | while | flops 8946946 | bytes 2429245 | solution.py:103
  38.4 0.9 constant_dynamic-slice_fusion.6
  39.8 0.2 fusion.81
  40.1 0.7 constant_dynamic-update-slice_fusion.2
  41.1 0.9 constant_dynamic-slice_fusion.6
  42.5 0.2 fusion.81
  42.8 0.7 constant_dynamic-update-slice_fusion.2
  43.8 0.9 constant_dynamic-slice_fusion.6
  45.5 0.7 constant_dynamic-update-slice_fusion.2
  46.5 0.9 constant_dynamic-slice_fusion.6
  48.1 0.7 constant_dynamic-update-slice_fusion.2
  49.1 0.9 constant_dynamic-slice_fusion.6
  50.6 0.2 fusion.81
  50.8 0.7 constant_dynamic-update-slice_fusion.2
  51.8 0.9 constant_dynamic-slice_fusion.6
  53.5 0.7 constant_dynamic-update-slice_fusion.2
  54.5 0.9 constant_dynamic-slice_fusion.6
  55.9 0.2 fusion.81
  56.2 0.7 constant_dynamic-update-slice_fusion.2
  57.2 0.9 constant_dynamic-slice_fusion.6
  58.9 0.7 constant_dynamic-update-slice_fusion.2
  59.6 1.4 %fusion.16 = bf16[8,32,256]{1,2,0:T(8,128)(2,1)S(1)} fusion(f32[8,32,256]{1,2,0:T(8,128)} %get-tuple-element.53, f32[8,32,8]{1,2,0:T(8,128)S(1)} %bitcast.137), kind=kLoop, calls=%fused_computation.38 | loop fusion | flops 131072 | bytes 401408 | tf_op jit(solution)/shard_map/convert_element_type | solution.py:107
  61.0 0.4 multiply_reduce_fusion.1
  61.5 0.3 copy-done.5
  62.0 0.7 copy.49
  62.8 4.7 %all-to-all-start.2 = ((bf16[8,32,256]{2,0,1:T(8,128)(2,1)}), bf16[8,32,256]{2,0,1:T(8,128)(2,1)S(1)}, u32[]{:S(2)}, u32[]{:S(2)}) async-start(bf16[8,32,256]{2,0,1:T(8,128)(2,1)} %copy.49), calls=%async_computation.2 | async-start | bytes 262144 | tf_op jit(solution)/shard_map/all_to_all | solution.py:115
  67.7 0.7 copy.47
  68.4 5.4 %all-to-all-done.2 = bf16[8,32,256]{2,0,1:T(8,128)(2,1)S(1)} async-done(((bf16[8,32,256]{2,0,1:T(8,128)(2,1)}), bf16[8,32,256]{2,0,1:T(8,128)(2,1)S(1)}, u32[]{:S(2)}, u32[]{:S(2)}) %all-to-all-start.2) | async-done | bytes 131104 | tf_op jit(solution)/shard_map/all_to_all | solution.py:115
  73.8 3.3 %all-to-all-start.1 = ((bf16[8,32,256]{2,0,1:T(8,128)(2,1)}), bf16[8,32,256]{2,0,1:T(8,128)(2,1)S(1)}, u32[]{:S(2)}, u32[]{:S(2)}) async-start(bf16[8,32,256]{2,0,1:T(8,128)(2,1)} %copy.47), calls=%async_computation.1 | async-start | bytes 262144 | tf_op jit(solution)/shard_map/all_to_all | solution.py:114
  77.3 0.7 copy.45
  78.1 5.0 %all-to-all-done.1 = bf16[8,32,256]{2,0,1:T(8,128)(2,1)S(1)} async-done(((bf16[8,32,256]{2,0,1:T(8,128)(2,1)}), bf16[8,32,256]{2,0,1:T(8,128)(2,1)S(1)}, u32[]{:S(2)}, u32[]{:S(2)}) %all-to-all-start.1) | async-done | bytes 131104 | tf_op jit(solution)/shard_map/all_to_all | solution.py:114
  83.0 3.3 %all-to-all-start = ((bf16[8,32,256]{2,0,1:T(8,128)(2,1)}), bf16[8,32,256]{2,0,1:T(8,128)(2,1)S(1)}, u32[]{:S(2)}, u32[]{:S(2)}) async-start(bf16[8,32,256]{2,0,1:T(8,128)(2,1)} %copy.45), calls=%async_computation | async-start | bytes 262144 | tf_op jit(solution)/shard_map/all_to_all | solution.py:116
  86.9 5.3 %all-to-all-done = bf16[8,32,256]{2,0,1:T(8,128)(2,1)S(1)} async-done(((bf16[8,32,256]{2,0,1:T(8,128)(2,1)}), bf16[8,32,256]{2,0,1:T(8,128)(2,1)S(1)}, u32[]{:S(2)}, u32[]{:S(2)}) %all-to-all-start) | async-done | bytes 131104 | tf_op jit(solution)/shard_map/all_to_all | solution.py:116
  92.5 0.9 fusion.57
  93.4 0.3 fusion.22
  93.7 0.8 fusion.11
  95.2 8.4 %all_to_all.50 = bf16[4,8,8,256]{3,2,1,0:T(8,128)(2,1)S(1)} all-to-all(bf16[4,8,8,256]{3,2,1,0:T(8,128)(2,1)S(1)} %pad_maximum_fusion), channel_id=1, replica_groups=mesh['lon'=8,'lat'=4] {'lat'}, dimensions={0} | all-to-all | bytes 262144 | tf_op jit(solution)/shard_map/all_to_all | solution.py:120
  103.6 0.3 multiply_reduce_fusion
  104.0 0.3 fusion.28
  104.3 0.6 copy-done.14
  105.1 1.2 %fusion.15 = bf16[8,32,256]{2,1,0:T(8,128)(2,1)} fusion(f32[8,32,256]{2,1,0:T(8,128)S(1)} %get-tuple-element.136, f32[8,32,1024]{2,1,0:T(8,128)S(1)} %fusion.28, bf16[1024,256]{1,0:T(8,128)(2,1)S(1)} %copy-done.14, bf16[256,1024]{1,0:T(8,128)(2,1)S(1)} %copy-done.15, f32[256]{0:T(256)S(1)} %copy-done.12, f32[8,32]{1,0:T(8,128)S(1)} %add_rsqrt_fusion), kind=kOutput, calls=%fused_computation.32 | convolution fusion | flops 270336000 | bytes 2492416 | tf_op jit(solution)/shard_map/dot_general | solution.py:128
  (134 shorter events, 10.7 us)
Async XLA Ops:
  6.5 97.4 %copy-start = (bf16[256,1024]{1,0:T(8,128)(2,1)S(1)}, bf16[256,1024]{1,0:T(8,128)(2,1)}, u32[]{:S(2)}) copy-start(bf16[256,1024]{1,0:T(8,128)(2,1)} %param.37) | copy-start | bytes 1572868
  6.5 5.1 %copy-start.16 = (f32[8]{0:T(128)S(1)}, f32[8]{0:T(128)}, u32[]{:S(2)}) copy-start(f32[8]{0:T(128)} %param.27) | copy-start | bytes 100
  6.5 5.1 %copy-start.13 = (f32[8]{0:T(128)S(1)}, f32[8]{0:T(128)}, u32[]{:S(2)}) copy-start(f32[8]{0:T(128)} %param.35) | copy-start | bytes 100
  6.5 29.1 %copy-start.3 = (bf16[256,256]{1,0:T(8,128)(2,1)S(1)}, bf16[256,256]{1,0:T(8,128)(2,1)}, u32[]{:S(2)}) copy-start(bf16[256,256]{1,0:T(8,128)(2,1)} %param.24) | copy-start | bytes 393220
  6.5 29.1 %all-gather.2.cloned.1.call-start = ((), (), s32[]{:S(2)}) async-start(), calls=%async_computation.4 | async-start | bytes 1179648 | tf_op jit(solution)/shard_map/all_gather | solution.py:70
  11.7 25.7 %copy-start.4 = (bf16[256,256]{1,0:T(8,128)(2,1)S(1)}, bf16[256,256]{1,0:T(8,128)(2,1)}, u32[]{:S(2)}) copy-start(bf16[256,256]{1,0:T(8,128)(2,1)} %param.25) | copy-start | bytes 393220
  35.6 1.8 %copy-start.1 = (bf16[8,256,256]{2,1,0:T(8,128)(2,1)S(1)}, bf16[8,256,256]{2,1,0:T(8,128)(2,1)}, u32[]{:S(2)}) copy-start(bf16[8,256,256]{2,1,0:T(8,128)(2,1)} %all-gather.2.cloned.1.call-done) | copy-start | bytes 3145732
  37.4 0.7 copy-start.10
  59.6 1.4 %copy-start.2 = (bf16[8,32,256]{2,1,0:T(8,128)(2,1)S(1)}, bf16[8,32,256]{2,1,0:T(8,128)(2,1)}, u32[]{:S(2)}) copy-start(bf16[8,32,256]{2,1,0:T(8,128)(2,1)} %param.21) | copy-start | bytes 393220
  59.6 1.4 %copy-start.9 = (bf16[256,256]{1,0:T(8,128)(2,1)S(1)}, bf16[256,256]{1,0:T(8,128)(2,1)}, u32[]{:S(2)}) copy-start(bf16[256,256]{1,0:T(8,128)(2,1)} %param.26) | copy-start | bytes 393220
  59.6 1.8 %copy-start.11 = (f32[256]{0:T(256)S(1)}, f32[256]{0:T(256)}, u32[]{:S(2)}) copy-start(f32[256]{0:T(256)} %param.29) | copy-start | bytes 3076
  60.9 0.9 copy-start.5
  61.0 6.6 %copy-start.6 = (bf16[256,256]{1,0:T(8,128)(2,1)S(1)}, bf16[256,256]{1,0:T(8,128)(2,1)}, u32[]{:S(2)}) copy-start(bf16[256,256]{1,0:T(8,128)(2,1)} %param.30) | copy-start | bytes 393220
  61.4 15.7 %copy-start.7 = (bf16[256,256]{1,0:T(8,128)(2,1)S(1)}, bf16[256,256]{1,0:T(8,128)(2,1)}, u32[]{:S(2)}) copy-start(bf16[256,256]{1,0:T(8,128)(2,1)} %param.32) | copy-start | bytes 393220
  62.8 23.6 %copy-start.17 = (f32[8]{0:T(128)S(1)}, f32[8]{0:T(128)}, u32[]{:S(2)}) copy-start(f32[8]{0:T(128)} %param.34) | copy-start | bytes 100
  62.8 11.0 %all-to-all-start.2 = ((bf16[8,32,256]{2,0,1:T(8,128)(2,1)}), bf16[8,32,256]{2,0,1:T(8,128)(2,1)S(1)}, u32[]{:S(2)}, u32[]{:S(2)}) async-start(bf16[8,32,256]{2,0,1:T(8,128)(2,1)} %copy.49), calls=%async_computation.2 | async-start | bytes 262144 | tf_op jit(solution)/shard_map/all_to_all | solution.py:115
  73.8 9.2 %all-to-all-start.1 = ((bf16[8,32,256]{2,0,1:T(8,128)(2,1)}), bf16[8,32,256]{2,0,1:T(8,128)(2,1)S(1)}, u32[]{:S(2)}, u32[]{:S(2)}) async-start(bf16[8,32,256]{2,0,1:T(8,128)(2,1)} %copy.47), calls=%async_computation.1 | async-start | bytes 262144 | tf_op jit(solution)/shard_map/all_to_all | solution.py:114
  83.0 9.2 %all-to-all-start = ((bf16[8,32,256]{2,0,1:T(8,128)(2,1)}), bf16[8,32,256]{2,0,1:T(8,128)(2,1)S(1)}, u32[]{:S(2)}, u32[]{:S(2)}) async-start(bf16[8,32,256]{2,0,1:T(8,128)(2,1)} %copy.45), calls=%async_computation | async-start | bytes 262144 | tf_op jit(solution)/shard_map/all_to_all | solution.py:116
  94.6 9.1 %copy-start.8 = (bf16[256,256]{1,0:T(8,128)(2,1)S(1)}, bf16[256,256]{1,0:T(8,128)(2,1)}, u32[]{:S(2)}) copy-start(bf16[256,256]{1,0:T(8,128)(2,1)} %param.33) | copy-start | bytes 393220
  94.9 9.1 %copy-start.12 = (f32[256]{0:T(256)S(1)}, f32[256]{0:T(256)}, u32[]{:S(2)}) copy-start(f32[256]{0:T(256)} %param.36) | copy-start | bytes 3076
  103.9 1.0 copy-start.14
  103.9 1.2 %copy-start.15 = (bf16[256,1024]{1,0:T(8,128)(2,1)S(1)}, bf16[256,1024]{1,0:T(8,128)(2,1)}, u32[]{:S(2)}) copy-start(bf16[256,1024]{1,0:T(8,128)(2,1)} %param.38) | copy-start | bytes 1572868
Sparse Core Ops, SparseCore 0:
  9.5 26.0 all-gather.1
